TPU v7x, 32 devices: a whole 2x2x4 slice. The times are simulated.
32 devices in a mesh: cell: 8 (over z, x), seq: 4 (over y, core).
Axes of the slice: x: 2, y: 2, z: 4, core: 2. Of those that a mesh axis runs over, the one named last changes fastest.
Arguments:
- cells_in: bfloat16 [8, 1024, 1120], P('cell', 'seq'), may hold values from -6 to 6
- dataset_ids: int32 [8], P('cell'), may hold values from 0 to 15
- cell_lengths: int32 [8], P('cell'), may hold values from 512 to 1024, as said below
- table: float32 [16, 1120], replicated, may hold values from -3 to 3
- wqkv: bfloat16 [1120, 3360], P('seq'), may hold values from -0.25 to 0.25
- bq: float32 [1120], replicated, may hold values from -3 to 3
- bv: float32 [1120], replicated, may hold values from -3 to 3
- wout: bfloat16 [1120, 1120], P('seq'), may hold values from -0.5 to 0.5
- bout: float32 [1120], replicated, may hold values from -2 to 2
- gain1: float32 [1120], replicated, may hold values from 0.1 to 1.9
- shift1: float32 [1120], replicated, may hold values from -2 to 2
- gain2: float32 [1120], replicated, may hold values from 0.1 to 1.9
- shift2: float32 [1120], replicated, may hold values from -2 to 2
- wup: bfloat16 [1120, 4480], P(None, 'cell'), may hold values from -0.1875 to 0.1875
- bup: float32 [4480], replicated, may hold values from -2 to 2
- wdown: bfloat16 [4480, 1120], P('cell'), may hold values from -0.09375 to 0.09375
- bdown: float32 [1120], replicated, may hold values from -2 to 2
- out_grad: bfloat16 [8, 1024, 1120], P('cell', 'seq'), may hold values from -6 to 6
Outputs:
- cells_out: bfloat16 [8, 1024, 1120], P('cell', 'seq')
- cells_grad: bfloat16 [8, 1024, 1120], P('cell', 'seq')
- grad_table: float32 [16, 1120], P(None, 'seq')
- grad_wqkv: float32 [1120, 3360], P('seq')
- grad_bq: float32 [1120], P('seq')
- grad_bv: float32 [1120], P('seq')
- grad_wout: float32 [1120, 1120], P('seq')
- grad_bout: float32 [1120], P('seq')
- grad_gain1: float32 [1120], P('seq')
- grad_shift1: float32 [1120], P('seq')
- grad_gain2: float32 [1120], P('seq')
- grad_shift2: float32 [1120], P('seq')
- grad_wup: float32 [1120, 4480], P(None, 'cell')
- grad_bup: float32 [4480], P('seq')
- grad_wdown: float32 [4480, 1120], P('cell')
- grad_bdown: float32 [1120], P('seq')
Inputs may be any that keep to these rules, and one draw needn't show every extreme that they name: `cell_lengths`: some cell has exactly 1024 live positions.
All inputs are finite; a program needn't handle non-finite values.
Results may differ from a plain program's by a relative error of at most 0.015.
Values may be sent and summed in bfloat16 or wider, within the bound.
A program may use at most 256 MiB of HBM per device.

v0:
```python
import math
import jax
import jax.numpy as jnp
from jax import lax
from jax.sharding import PartitionSpec as P

HEAD_DIM = 56
norm_eps = 1e-05


def cut_along(x, dim, size):
    lengths = x.shape
    parts = x.reshape(*lengths[:dim], size, lengths[dim] // size, *lengths[dim + 1 :])
    return jnp.moveaxis(parts, dim, 0)


def sent_and_summed(x, axis, dim):
    parts = cut_along(x, dim, lax.axis_size(axis))
    arrived = lax.all_to_all(parts, axis, split_axis=0, concat_axis=0, tiled=True)
    return arrived.astype(jnp.float32).sum(axis=0)


def product(left, right):
    return jnp.dot(left, right, preferred_element_type=jnp.float32)


def left_inner(left, right):
    return lax.dot_general(
        left, right, (((0,), (0,)), ((), ())), preferred_element_type=jnp.float32
    )


def right_inner(left, right):
    return lax.dot_general(
        left, right, (((1,), (1,)), ((), ())), preferred_element_type=jnp.float32
    )


def norm_forward(hidden, gain, shift):
    centre = hidden - jnp.mean(hidden, axis=-1, keepdims=True)
    inverse = lax.rsqrt(jnp.mean(centre * centre, axis=-1, keepdims=True) + norm_eps)
    unit_rows = centre * inverse
    return (unit_rows * gain + shift, unit_rows, inverse)


def norm_backward(grad_rows, unit_rows, inverse, gain):
    scaled = grad_rows * gain
    inside = (
        scaled
        - jnp.mean(scaled, axis=-1, keepdims=True)
        - unit_rows * jnp.mean(scaled * unit_rows, axis=-1, keepdims=True)
    )
    return (inside * inverse, jnp.sum(grad_rows * unit_rows, axis=0), jnp.sum(grad_rows, axis=0))


def block_scores(queries, keys_used, first_row, length, score_scale):
    row_count = queries.shape[0]
    key_count = keys_used.shape[0]
    scores = (
        jnp.einsum("qhd,khd->hqk", queries, keys_used, preferred_element_type=jnp.float32)
        * score_scale
    )
    query_pos = first_row + lax.broadcasted_iota(jnp.int32, (row_count, key_count), 0)
    key_pos = lax.broadcasted_iota(jnp.int32, (row_count, key_count), 1)
    visible = (key_pos <= query_pos) & (key_pos < length)
    return jnp.where(visible[None], scores, -1e30)


def attend_forward(query_heads, key_heads, value_heads, length, row_block, score_scale):
    slot_count = query_heads.shape[0]
    outputs = []
    logsums = []
    for block_idx in range(slot_count // row_block):
        first_row = block_idx * row_block
        key_count = first_row + row_block
        scores = block_scores(
            query_heads[first_row:key_count], key_heads[:key_count], first_row, length, score_scale
        )
        highest = jnp.max(scores, axis=-1, keepdims=True)
        weights = jnp.exp(scores - highest)
        denominator = jnp.sum(weights, axis=-1, keepdims=True)
        prob_low = (weights / denominator).astype(jnp.bfloat16)
        outputs.append(
            jnp.einsum(
                "hqk,khd->qhd",
                prob_low,
                value_heads[:key_count],
                preferred_element_type=jnp.float32,
            )
        )
        logsums.append(highest + jnp.log(denominator))
    return (jnp.concatenate(outputs, axis=0), logsums)


def attend_backward(
    query_heads, key_heads, value_heads, grad_heads, logsums, length, row_block, score_scale
):
    slot_count = query_heads.shape[0]
    grad_query = []
    grad_key = jnp.zeros(key_heads.shape, jnp.float32)
    grad_value = jnp.zeros(value_heads.shape, jnp.float32)
    for block_idx in range(slot_count // row_block):
        first_row = block_idx * row_block
        key_count = first_row + row_block
        queries = query_heads[first_row:key_count]
        grads_here = grad_heads[first_row:key_count]
        scores = block_scores(queries, key_heads[:key_count], first_row, length, score_scale)
        prob_full = jnp.exp(scores - logsums[block_idx])
        prob_low = prob_full.astype(jnp.bfloat16)
        grad_prob = jnp.einsum(
            "qhd,khd->hqk", grads_here, value_heads[:key_count], preferred_element_type=jnp.float32
        )
        grad_value = grad_value.at[:key_count].add(
            jnp.einsum("hqk,qhd->khd", prob_low, grads_here, preferred_element_type=jnp.float32)
        )
        row_inner = jnp.sum(prob_full * grad_prob, axis=-1, keepdims=True)
        grad_score = (prob_full * (grad_prob - row_inner)).astype(jnp.bfloat16)
        grad_query.append(
            jnp.einsum(
                "hqk,khd->qhd",
                grad_score,
                key_heads[:key_count],
                preferred_element_type=jnp.float32,
            )
            * score_scale
        )
        grad_key = grad_key.at[:key_count].add(
            jnp.einsum("hqk,qhd->khd", grad_score, queries, preferred_element_type=jnp.float32)
            * score_scale
        )
    return (jnp.concatenate(grad_query, axis=0), grad_key, grad_value)


def shards(
    cells_in,
    dataset_ids,
    cell_lengths,
    table,
    wqkv,
    bq,
    bv,
    wout,
    bout,
    gain1,
    shift1,
    gain2,
    shift2,
    wup,
    bup,
    wdown,
    bdown,
    out_grad,
):
    seq_count = lax.axis_size("seq")
    local_rows = cells_in.shape[1]
    width = cells_in.shape[2]
    slot_count = local_rows * seq_count
    group_width = width // seq_count
    heads_here = group_width // HEAD_DIM
    row_block = min(512, slot_count)
    score_scale = 1.0 / math.sqrt(HEAD_DIM)
    length = cell_lengths[0]
    dataset_pick = (
        lax.broadcasted_iota(jnp.int32, (1, table.shape[0]), 1) == dataset_ids[0]
    ).astype(jnp.float32)
    table_row = jnp.dot(
        dataset_pick, table, precision=lax.Precision.HIGHEST, preferred_element_type=jnp.float32
    )
    resid_in = cells_in[0].astype(jnp.float32) + table_row
    normed1, unit1, inverse1 = norm_forward(resid_in, gain1, shift1)
    normed1_low = normed1.astype(jnp.bfloat16)
    wqkv_full, wout_full = (
        lax.all_gather(wqkv, "seq", axis=0, tiled=True),
        lax.all_gather(wout, "seq", axis=0, tiled=True),
    )
    qkv_bias = jnp.concatenate([bq, jnp.zeros_like(bq), bv])
    qkv_low = (product(normed1_low, wqkv_full) + qkv_bias).astype(jnp.bfloat16)
    qkv_heads = lax.all_to_all(
        qkv_low.reshape(local_rows, 3, seq_count, group_width),
        "seq",
        split_axis=2,
        concat_axis=0,
        tiled=True,
    )
    query_heads = qkv_heads[:, 0, 0].reshape(slot_count, heads_here, HEAD_DIM)
    key_heads = qkv_heads[:, 1, 0].reshape(slot_count, heads_here, HEAD_DIM)
    value_heads = qkv_heads[:, 2, 0].reshape(slot_count, heads_here, HEAD_DIM)
    context, logsums = attend_forward(
        query_heads, key_heads, value_heads, length, row_block, score_scale
    )
    context_low = context.astype(jnp.bfloat16).reshape(slot_count, 1, group_width)
    context_rows = lax.all_to_all(
        context_low, "seq", split_axis=0, concat_axis=1, tiled=True
    ).reshape(local_rows, width)
    resid_mid = resid_in + product(context_rows, wout_full) + bout
    normed2, unit2, inverse2 = norm_forward(resid_mid, gain2, shift2)
    normed2_low = normed2.astype(jnp.bfloat16)
    wup_full, wdown_full = (
        lax.all_gather(wup, "cell", axis=1, tiled=True),
        lax.all_gather(wdown, "cell", axis=0, tiled=True),
    )
    up_rows = product(normed2_low, wup_full) + bup
    act_low = jax.nn.gelu(up_rows, approximate=True).astype(jnp.bfloat16)
    cells_out = (resid_mid + product(act_low, wdown_full) + bdown).astype(jnp.bfloat16)[None]
    grad_out = out_grad[0]
    grad_rows = grad_out.astype(jnp.float32)
    grad_bdown = jnp.sum(grad_rows, axis=0)
    grad_wdown = left_inner(act_low, grad_out)
    wup_back, wdown_back = (
        lax.all_gather(wup, "cell", axis=1, tiled=True),
        lax.all_gather(wdown, "cell", axis=0, tiled=True),
    )
    grad_act = right_inner(grad_out, wdown_back)
    gelu_pull = jax.vjp(lambda values: jax.nn.gelu(values, approximate=True), up_rows)[1]
    grad_up_low = gelu_pull(grad_act)[0].astype(jnp.bfloat16)
    grad_bup = jnp.sum(grad_up_low.astype(jnp.float32), axis=0)
    grad_wup = left_inner(normed2_low, grad_up_low)
    grad_norm2 = right_inner(grad_up_low, wup_back)
    back_second, grad_gain2, grad_shift2 = norm_backward(grad_norm2, unit2, inverse2, gain2)
    grad_mid = grad_rows + back_second
    grad_mid_low = grad_mid.astype(jnp.bfloat16)
    grad_bout = jnp.sum(grad_mid_low.astype(jnp.float32), axis=0)
    grad_context = right_inner(grad_mid_low, wout_full).astype(jnp.bfloat16)
    grad_context_heads = lax.all_to_all(
        grad_context.reshape(local_rows, seq_count, group_width),
        "seq",
        split_axis=1,
        concat_axis=0,
        tiled=True,
    ).reshape(slot_count, heads_here, HEAD_DIM)
    grad_query, grad_key, grad_value = attend_backward(
        query_heads,
        key_heads,
        value_heads,
        grad_context_heads,
        logsums,
        length,
        row_block,
        score_scale,
    )
    grad_qkv_heads = jnp.stack([grad_query, grad_key, grad_value], axis=1).astype(jnp.bfloat16)
    grad_qkv = lax.all_to_all(
        grad_qkv_heads.reshape(slot_count, 3, 1, group_width),
        "seq",
        split_axis=0,
        concat_axis=2,
        tiled=True,
    ).reshape(local_rows, 3 * width)
    grad_qkv_wide = grad_qkv.astype(jnp.float32)
    grad_bq = jnp.sum(grad_qkv_wide[:, :width], axis=0)
    grad_bv = jnp.sum(grad_qkv_wide[:, 2 * width :], axis=0)
    grad_norm1 = right_inner(grad_qkv, wqkv_full)
    back_first, grad_gain1, grad_shift1 = norm_backward(grad_norm1, unit1, inverse1, gain1)
    grad_in = grad_mid + back_first
    cells_grad = grad_in.astype(jnp.bfloat16)[None]
    grad_table = jnp.transpose(dataset_pick) * jnp.sum(grad_in, axis=0)[None, :]
    grad_wqkv = left_inner(normed1_low, grad_qkv)
    grad_wout = left_inner(context_rows, grad_mid_low)
    seq_parts = (
        lax.psum_scatter(
            grad_table.astype(jnp.bfloat16), "seq", scatter_dimension=1, tiled=True
        ).astype(jnp.float32),
        lax.psum_scatter(
            grad_wqkv.astype(jnp.bfloat16), "seq", scatter_dimension=0, tiled=True
        ).astype(jnp.float32),
        lax.psum_scatter(
            grad_wout.astype(jnp.bfloat16), "seq", scatter_dimension=0, tiled=True
        ).astype(jnp.float32),
        lax.psum_scatter(
            grad_bq.astype(jnp.bfloat16), "seq", scatter_dimension=0, tiled=True
        ).astype(jnp.float32),
        lax.psum_scatter(
            grad_bv.astype(jnp.bfloat16), "seq", scatter_dimension=0, tiled=True
        ).astype(jnp.float32),
        lax.psum_scatter(
            grad_bout.astype(jnp.bfloat16), "seq", scatter_dimension=0, tiled=True
        ).astype(jnp.float32),
        lax.psum_scatter(
            grad_gain1.astype(jnp.bfloat16), "seq", scatter_dimension=0, tiled=True
        ).astype(jnp.float32),
        lax.psum_scatter(
            grad_shift1.astype(jnp.bfloat16), "seq", scatter_dimension=0, tiled=True
        ).astype(jnp.float32),
        lax.psum_scatter(
            grad_gain2.astype(jnp.bfloat16), "seq", scatter_dimension=0, tiled=True
        ).astype(jnp.float32),
        lax.psum_scatter(
            grad_shift2.astype(jnp.bfloat16), "seq", scatter_dimension=0, tiled=True
        ).astype(jnp.float32),
        lax.psum_scatter(
            grad_bup.astype(jnp.bfloat16), "seq", scatter_dimension=0, tiled=True
        ).astype(jnp.float32),
        lax.psum_scatter(
            grad_bdown.astype(jnp.bfloat16), "seq", scatter_dimension=0, tiled=True
        ).astype(jnp.float32),
    )
    share_qkv = seq_parts[1]
    share_out = seq_parts[2]
    part_qkv, part_out = (
        sent_and_summed(share_qkv.reshape(-1).astype(jnp.bfloat16), "cell", 0),
        sent_and_summed(share_out.reshape(-1).astype(jnp.bfloat16), "cell", 0),
    )
    whole_qkv, whole_out = (
        lax.all_gather(part_qkv.astype(jnp.bfloat16), "cell", axis=0, tiled=True).astype(
            part_qkv.dtype
        ),
        lax.all_gather(part_out.astype(jnp.bfloat16), "cell", axis=0, tiled=True).astype(
            part_out.dtype
        ),
    )
    total_wqkv = whole_qkv.reshape(share_qkv.shape)
    total_wout = whole_out.reshape(share_out.shape)
    others = lax.psum((seq_parts[0],) + tuple(seq_parts[3:]), "cell")
    summed = (others[0], total_wqkv, total_wout) + tuple(others[1:])
    cell_up, cell_down = (
        lax.psum_scatter(grad_wup, "cell", scatter_dimension=1, tiled=True),
        lax.psum_scatter(grad_wdown, "cell", scatter_dimension=0, tiled=True),
    )
    total_up, total_down = (
        lax.psum(cell_up.astype(jnp.bfloat16), "seq").astype(jnp.float32),
        lax.psum(cell_down.astype(jnp.bfloat16), "seq").astype(jnp.float32),
    )
    return (
        cells_out,
        cells_grad,
        summed[0],
        summed[1],
        summed[3],
        summed[4],
        summed[2],
        summed[5],
        summed[6],
        summed[7],
        summed[8],
        summed[9],
        total_up,
        summed[10],
        total_down,
        summed[11],
    )


def solution(mesh):
    return jax.shard_map(
        shards,
        mesh=mesh,
        in_specs=(
            P("cell", "seq", None),
            P("cell"),
            P("cell"),
            P(),
            P("seq", None),
            P(),
            P(),
            P("seq", None),
            P(),
            P(),
            P(),
            P(),
            P(),
            P(None, "cell"),
            P(),
            P("cell", None),
            P(),
            P("cell", "seq", None),
        ),
        out_specs=(
            P("cell", "seq", None),
            P("cell", "seq", None),
            P(None, "seq"),
            P("seq", None),
            P("seq"),
            P("seq"),
            P("seq", None),
            P("seq"),
            P("seq"),
            P("seq"),
            P("seq"),
            P("seq"),
            P(None, "cell"),
            P("seq"),
            P("cell", None),
            P("seq"),
        ),
        check_vma=False,
    )
```

profile of v0, /device:TPU:0, one launch (start us, length us, event | category | flops | bytes accessed | tf_op | source)
XLA Modules:
  0.0 1535.5 jit_solution(6749002238563494380)
XLA Ops:
  11.5 55.4 %all-gather.5.cloned.1.call-done = bf16[1120,3360]{1,0:T(8,128)(2,1)} async-done(((bf16[280,3360]{1,0:T(8,128)(2,1)}), bf16[1120,3360]{1,0:T(8,128)(2,1)}) %all-gather.5.cloned.1.call-update) | async-done | bytes 7526416 | tf_op jit(solution)/shard_map/all_gather | solution.py:173
  67.0 7.2 fusion.6
  81.1 29.6 %all-to-all-done = bf16[256,3,4,280]{0,3,1,2:T(8,128)(2,1)S(1)} async-done(((bf16[256,3,4,280]{0,3,1,2:T(8,128)(2,1)}), bf16[256,3,4,280]{0,3,1,2:T(8,128)(2,1)S(1)}, u32[]{:S(2)}, u32[]{:S(2)}) %all-to-all-start) | async-done | bytes 1720352 | tf_op jit(solution)/shard_map/all_to_all | solution.py:178
  131.0 9.3 all-to-all-done.1
  148.6 106.2 %all-gather.9.cloned.1.call-done = bf16[1120,4480]{0,1:T(8,128)(2,1)} async-done(((bf16[1120,560]{0,1:T(8,128)(2,1)}), bf16[1120,4480]{0,1:T(8,128)(2,1)}) %all-gather.9.cloned.1.call-update) | async-done | bytes 10035216 | tf_op jit(solution)/shard_map/all_gather | solution.py:199
  254.8 9.8 convolution_add_fusion
  264.6 138.9 %all-gather.11.cloned.1.call-done = bf16[4480,1120]{1,0:T(8,128)(2,1)} async-done(((bf16[560,1120]{1,0:T(8,128)(2,1)}), bf16[4480,1120]{1,0:T(8,128)(2,1)}) %all-gather.11.cloned.1.call-update) | async-done | bytes 10035216 | tf_op jit(solution)/shard_map/all_gather | solution.py:200
  403.6 12.7 fusion.104
  416.3 10.1 multiply_reduce_fusion.2
  435.9 6.7 all-to-all-done.2
  446.9 6.0 multiply_reduce_fusion.1
  453.3 5.9 fusion.33
  462.3 5.6 multiply_convert_fusion.1
  469.6 5.7 multiply_reduce_fusion
  496.6 7.6 pad_maximum_fusion
  504.2 39.4 %all_to_all.75 = bf16[1024,3,1,280]{3,1,2,0:T(4,128)(2,1)S(1)} all-to-all(bf16[1024,3,1,280]{3,1,2,0:T(4,128)(2,1)S(1)} %pad_maximum_fusion), channel_id=1, replica_groups=mesh['cell'=8,'seq'=4] {'seq'}, dimensions={0} | all-to-all | bytes 3440640 | tf_op jit(solution)/shard_map/all_to_all | solution.py:242
  555.4 14.6 fusion.95
  570.1 13.7 fusion.73
  587.3 6.2 reduce.20
  600.9 20.7 %reduce-scatter.14.cloned.1.call-done = bf16[280,3360]{1,0:T(8,128)(2,1)} async-done(((bf16[1120,3360]{1,0:T(8,128)(2,1)}), bf16[280,3360]{1,0:T(8,128)(2,1)}) %reduce-scatter.14.cloned.1.call-update) | async-done | bytes 1881616
  632.6 42.0 %reduce.19 = bf16[8,117600]{1,0:T(8,128)(2,1)} reduce(bf16[8,1,117600]{2,1,0:T(2,128)(2,1)} %convert_element_type.245, bf16[]{:T(256)} %broadcast.342), dimensions={1}, to_apply=%convert_element_type.245.reduce_sub_computation | reduce | bytes 3763202 | tf_op jit(solution)/shard_map/convert_element_type | solution.py:300
  700.5 73.5 %all-to-all-done.4 = bf16[8,2,58800]{2,1,0:T(2,128)(2,1)} async-done(((bf16[8,2,58800]{2,1,0:T(2,128)(2,1)}), bf16[8,2,58800]{2,1,0:T(2,128)(2,1)}, u32[]{:S(2)}, u32[]{:S(2)}) %all-to-all-start.4) | async-done | bytes 1881632 | tf_op jit(solution)/shard_map/all_to_all | solution.py:19
  774.0 7.9 reshape.517
  781.9 6.5 reduce_sum.244
  794.8 11.3 fusion.23
  808.2 5.9 fusion.62
  815.6 188.3 %reduce-scatter.10.cloned.1.call-done = f32[1120,560]{0,1:T(8,128)} async-done(((f32[1120,4480]{0,1:T(8,128)}), f32[1120,560]{0,1:T(8,128)}) %reduce-scatter.10.cloned.1.call-update) | async-done | bytes 2508816 | tf_op jit(solution)/shard_map/reduce_scatter | solution.py:316
  1006.9 336.9 %reduce-scatter.12.cloned.1.call-done = f32[560,1120]{1,0:T(8,128)} async-done(((f32[4480,1120]{1,0:T(8,128)}), f32[560,1120]{1,0:T(8,128)}) %reduce-scatter.12.cloned.1.call-update) | async-done | bytes 2508816 | tf_op jit(solution)/shard_map/reduce_scatter | solution.py:317
  1347.4 12.6 all-reduce.18
  1360.8 38.1 %all-reduce.16 = (f32[16,280]{1,0:T(8,128)}, f32[280]{0:T(512)}, f32[280]{0:T(512)}, f32[280]{0:T(512)}, f32[280]{0:T(512)}, /*index=5*/f32[280]{0:T(512)}, f32[...) all-reduce(f32[16,280]{1,0:T(8,128)S(1)} %dynamic-slice_convert_fus, ...), channel_id=1, replica_groups=mesh['cell'=8,'seq'=4] {'cell'}, use_global_device_ids=true, to_apply=%region_16.17 | all-reduce | flops 7840 | bytes 62720 | tf_op jit(solution)/shard_map/psum | solution.py:313
  1399.0 63.3 %all-reduce.23.cloned.1.call-done = (bf16[940800]{0:T(1024)(128)(2,1)}, bf16[313600]{0:T(1024)(128)(2,1)}) async-done(((bf16[940800]{0:T(1024)(128)(2,1)}, bf16[313600]{0:T(1024)(128)(2,1)}), (bf16[940800]{0:T(1024)(128)(2,1)}, bf16[313600]{0:T(1024)(128)(2,1)})) %all-reduce.23.cloned.1.call-update) | async-done | bytes 2508816
  1469.6 54.1 %all-reduce.25.cloned.1.call-done = (bf16[1120,560]{0,1:T(8,128)(2,1)}, bf16[560,1120]{1,0:T(8,128)(2,1)}) async-done(((bf16[1120,560]{0,1:T(8,128)(2,1)}, bf16[560,1120]{1,0:T(8,128)(2,1)}), (bf16[1120,560]{0,1:T(8,128)(2,1)}, bf16[560,1120]{1,0:T(8,128)(2,1)})) %all-reduce.25.cloned.1.call-update) | async-done | bytes 2508816 | tf_op jit(solution)/shard_map/psum | solution.py:320
  (237 shorter events, 164.6 us)
Async XLA Ops:
  7.2 59.7 %all-gather.5.cloned.1.call-start = ((), (), s32[]{:S(2)}) async-start(), calls=%async_computation.10 | async-start | bytes 9676800 | tf_op jit(solution)/shard_map/all_gather | solution.py:173
  8.0 59.0 %copy-start.35 = (f32[1120]{0:T(1024)S(1)}, f32[1120]{0:T(1024)}, u32[]{:S(2)}) copy-start(f32[1120]{0:T(1024)} %param.39) | copy-start | bytes 13444
  8.0 59.0 %copy-start.36 = (f32[1120]{0:T(1024)S(1)}, f32[1120]{0:T(1024)}, u32[]{:S(2)}) copy-start(f32[1120]{0:T(1024)} %param.40) | copy-start | bytes 13444
  8.0 137.0 %all-gather.7.cloned.1.call-start = ((), (), s32[]{:S(2)}) async-start(), calls=%async_computation.11 | async-start | bytes 3225600 | tf_op jit(solution)/shard_map/all_gather | solution.py:174
  8.7 246.1 %all-gather.9.cloned.1.call-start = ((), (), s32[]{:S(2)}) async-start(), calls=%async_computation.12 | async-start | bytes 11612160 | tf_op jit(solution)/shard_map/all_gather | solution.py:199
  9.5 394.1 %all-gather.11.cloned.1.call-start = ((), (), s32[]{:S(2)}) async-start(), calls=%async_computation.13 | async-start | bytes 11612160 | tf_op jit(solution)/shard_map/all_gather | solution.py:200
  11.5 62.7 %copy-start.39 = (f32[256]{0:T(256)}, f32[256]{0:T(256)S(1)}, u32[]{:S(2)}) copy-start(f32[256]{0:T(256)S(1)} %add_rsqrt_fusion.1) | copy-start | bytes 3076
  75.5 35.3 %all-to-all-start = ((bf16[256,3,4,280]{0,3,1,2:T(8,128)(2,1)}), bf16[256,3,4,280]{0,3,1,2:T(8,128)(2,1)S(1)}, u32[]{:S(2)}, u32[]{:S(2)}) async-start(bf16[256,3,4,280]{0,3,1,2:T(8,128)(2,1)} %copy.78), calls=%async_computation | async-start | bytes 3440640 | tf_op jit(solution)/shard_map/all_to_all | solution.py:178
  111.1 7.3 copy-start.29
  111.2 8.2 copy-start.23
  127.3 13.0 all-to-all-start.1
  145.0 109.8 %copy-start.33 = (f32[1120]{0:T(1024)S(1)}, f32[1120]{0:T(1024)}, u32[]{:S(2)}) copy-start(f32[1120]{0:T(1024)} %param.41) | copy-start | bytes 13444
  145.0 109.8 %copy-start.34 = (f32[1120]{0:T(1024)S(1)}, f32[1120]{0:T(1024)}, u32[]{:S(2)}) copy-start(f32[1120]{0:T(1024)} %param.42) | copy-start | bytes 13444
  145.0 109.8 %copy-start.48 = (f32[4480]{0:T(1024)S(1)}, f32[4480]{0:T(1024)}, u32[]{:S(2)}) copy-start(f32[4480]{0:T(1024)} %param.44) | copy-start | bytes 53764
  148.4 278.0 %copy-start.7 = (f32[256,1120]{0,1:T(8,128)}, f32[256,1120]{0,1:T(8,128)S(1)}, u32[]{:S(2)}) copy-start(f32[256,1120]{0,1:T(8,128)S(1)} %get-tuple-element.131) | copy-start | bytes 3440644
  148.6 277.8 %copy-start.37 = (f32[256]{0:T(256)}, f32[256]{0:T(256)S(1)}, u32[]{:S(2)}) copy-start(f32[256]{0:T(256)S(1)} %add_rsqrt_fusion) | copy-start | bytes 3076
  148.6 255.0 %copy-start.14 = (bf16[1,256,1120]{1,2,0:T(8,128)(2,1)S(1)}, bf16[1,256,1120]{1,2,0:T(8,128)(2,1)}, u32[]{:S(2)}) copy-start(bf16[1,256,1120]{1,2,0:T(8,128)(2,1)} %param.47) | copy-start | bytes 1720324
  416.3 10.1 copy-start.22
  429.9 12.8 all-to-all-start.2
  433.3 150.5 %reduce-scatter.16.cloned.1.call-start = ((), (), s32[]{:S(2)}) async-start(), calls=%async_computation.17 | async-start | bytes 3225600
  435.9 185.7 %reduce-scatter.14.cloned.1.call-start = ((), (), s32[]{:S(2)}) async-start(), calls=%async_computation.16 | async-start | bytes 9676800
  462.3 7.3 copy-start.18
  462.3 7.3 copy-start.24
  467.9 7.5 slice-start
  554.2 449.7 %reduce-scatter.10.cloned.1.call-start = ((), (), s32[]{:S(2)}) async-start(), calls=%async_computation.14 | async-start | bytes 23224320 | tf_op jit(solution)/shard_map/reduce_scatter | solution.py:316
  570.0 773.7 %reduce-scatter.12.cloned.1.call-start = ((), (), s32[]{:S(2)}) async-start(), calls=%async_computation.15 | async-start | bytes 23224320 | tf_op jit(solution)/shard_map/reduce_scatter | solution.py:317
  596.0 83.2 %all-to-all-start.5 = ((bf16[8,2,19600]{2,1,0:T(2,128)(2,1)}), bf16[8,2,19600]{2,1,0:T(2,128)(2,1)}, u32[]{:S(2)}, u32[]{:S(2)}) async-start(bf16[8,2,19600]{2,1,0:T(2,128)(2,1)} %reshape.518), calls=%async_computation.5 | async-start | bytes 1261568 | tf_op jit(solution)/shard_map/all_to_all | solution.py:19
  679.2 9.0 copy-start.51
  679.2 94.8 %all-to-all-start.4 = ((bf16[8,2,58800]{2,1,0:T(2,128)(2,1)}), bf16[8,2,58800]{2,1,0:T(2,128)(2,1)}, u32[]{:S(2)}, u32[]{:S(2)}) async-start(bf16[8,2,58800]{2,1,0:T(2,128)(2,1)} %reshape.516), calls=%async_computation.4 | async-start | bytes 3768320 | tf_op jit(solution)/shard_map/all_to_all | solution.py:19
  684.7 777.5 %all-reduce.23.cloned.1.call-start = ((), (), s32[]{:S(2)}) async-start(), calls=%async_computation.18 | async-start | bytes 5021696
  794.6 729.1 %all-reduce.25.cloned.1.call-start = ((), (), s32[]{:S(2)}) async-start(), calls=%async_computation.19 | async-start | bytes 5160960 | tf_op jit(solution)/shard_map/psum | solution.py:320
  1006.9 339.9 %copy-start.11 = (f32[256,3360]{0,1:T(8,128)S(1)}, f32[256,3360]{0,1:T(8,128)}, u32[]{:S(2)}) copy-start(f32[256,3360]{0,1:T(8,128)} %convert_element_type.222) | copy-start | bytes 10321924
  (39 other events, 137.6 us)
Sparse Core Ops, SparseCore 0:
  9.6 57.3 all-gather.4
  68.5 35.2 all-gather.6
  106.0 148.7 all-gather.8
  256.9 146.6 all-gather.10
  437.0 33.1 reduce-scatter.15
  554.3 67.1 reduce-scatter.13
  625.5 378.4 reduce-scatter.9
  1007.9 335.8 reduce-scatter.11
  1348.6 113.6 all-reduce.22
  1465.2 58.4 all-reduce.24
where the time goes:
time: 1540 us
  waiting for transfers between devices  1090 us (71%)
  matrix products  136 us (9%)
  other arithmetic  98.1 us (6%)
  blocking collectives  90.2 us (6%)
  local copies, waits for them, and re-layouts  83.7 us (5%)
  starting transfers between devices  22.3 us (1%)
  between operations  19.2 us (1%)
    reduce_scatter x1, waiting for transfers between devices, shards(): lax.psum_scatter(grad_wdown, 'cell', scatter_dimension=0, tiled=True)  337 us
    reduce_scatter x1, waiting for transfers between devices, shards(): lax.psum_scatter(grad_wup, 'cell', scatter_dimension=1, tiled=True)  188 us
    all_gather x1, waiting for transfers between devices, shards(): lax.all_gather(wdown, 'cell', axis=0, tiled=True)  139 us
    all_gather x1, waiting for transfers between devices, shards(): lax.all_gather(wup, 'cell', axis=1, tiled=True)  106 us
    unnamed x13, waiting for transfers between devices  86.7 us
    all_to_all x2, waiting for transfers between devices, sent_and_summed(): lax.all_to_all(parts, axis, split_axis=0, concat_axis=0, tiled=True)  73.5 us
    all_gather x1, waiting for transfers between devices, shards(): lax.all_gather(wqkv, 'seq', axis=0, tiled=True)  55.4 us
    psum x1, waiting for transfers between devices, shards(): lax.psum(cell_up.astype(jnp.bfloat16), 'seq').astype(jnp.float32)  54.1 us
  transfers between devices with their start and end apart: 15, of which 12 were waited for; matrix products, arithmetic and copies ran while one was open for 18% of the time, Pallas kernels for 0%

commit v1 on v0

--- a/solution.py
+++ b/solution.py
@@ -6,6 +6,35 @@
 
 HEAD_DIM = 56
 norm_eps = 1e-05
+
+
+def group_the_bench(sheet, dim_k, w_in):
+    spare = sheet.shape
+    d_next = sheet.reshape(*spare[:dim_k], w_in, spare[dim_k] // w_in, *spare[dim_k + 1 :])
+    return jnp.moveaxis(d_next, dim_k, 0)
+
+
+def wrap_the_face(m, d0):
+    m = jnp.moveaxis(m, 0, d0)
+    y_new = m.shape
+    return m.reshape(*y_new[:d0], y_new[d0] * y_new[d0 + 1], *y_new[d0 + 2 :])
+
+
+def lead_figure(original, shard_axis, local_values, content):
+    seen_now, frame_out = (jax.lax.axis_size(shard_axis), jax.lax.axis_index(shard_axis))
+    t1 = group_the_bench(original, local_values, seen_now)
+    made = [t1[frame_out]]
+    dev_j = 1
+    while dev_j < seen_now:
+        passed = t1[frame_out ^ dev_j]
+        made.append(
+            jax.lax.ppermute(
+                passed, axis_name=shard_axis, perm=[(it, it ^ dev_j) for it in range(seen_now)]
+            )
+        )
+        dev_j = dev_j + 1
+    t1 = jnp.stack(made, axis=0)[frame_out ^ jnp.arange(seen_now)]
+    return wrap_the_face(t1, content)
 
 
 def cut_along(x, dim, size):
@@ -239,12 +268,8 @@
         score_scale,
     )
     grad_qkv_heads = jnp.stack([grad_query, grad_key, grad_value], axis=1).astype(jnp.bfloat16)
-    grad_qkv = lax.all_to_all(
-        grad_qkv_heads.reshape(slot_count, 3, 1, group_width),
-        "seq",
-        split_axis=0,
-        concat_axis=2,
-        tiled=True,
+    grad_qkv = lead_figure(
+        grad_qkv_heads.reshape(slot_count, 3, 1, group_width), "seq", 0, 2
     ).reshape(local_rows, 3 * width)
     grad_qkv_wide = grad_qkv.astype(jnp.float32)
     grad_bq = jnp.sum(grad_qkv_wide[:, :width], axis=0)

time: 1540 us -> 1500 us (0.974)
  blocking collectives: 90.2 us -> 50.7 us
  waiting for transfers between devices: 1090 us -> 1110 us
    all_to_all x1 -> x0, blocking collectives: 39.4 us -> none  [shards(): lax.all_to_all(grad_qkv_heads.reshape(slot_count, 3, 1, group_width), 'se...]
    ppermute x0 -> x3, waiting for transfers between devices: none -> 19.1 us  [lead_figure(): jax.lax.ppermute(passed, axis_name=shard_axis, perm=[(it, it ^ dev_j) for...]
    unnamed x126 -> x134, local copies, waits for them, and re-layouts: 43.3 us -> 46.1 us
  transfers between devices with their start and end apart: 15 -> 18, of which waited for: 12 -> 14; matrix products, arithmetic and copies ran while one was open for 18% -> 17% of each run, Pallas kernels for 0% -> 0%
where the time goes in v1:
time: 1500 us; the launch traced here: 1490 us
  waiting for transfers between devices  1110 us (74%)
  matrix products  128 us (9%)
  other arithmetic  87.2 us (6%)
  local copies, waits for them, and re-layouts  73.2 us (5%)
  blocking collectives  50.7 us (3%)
  starting transfers between devices  24.6 us (2%)
  between operations  19.3 us (1%)
    reduce_scatter x1, waiting for transfers between devices, shards(): lax.psum_scatter(grad_wdown, 'cell', scatter_dimension=0, tiled=True)  337 us
    reduce_scatter x1, waiting for transfers between devices, shards(): lax.psum_scatter(grad_wup, 'cell', scatter_dimension=1, tiled=True)  189 us
    all_gather x1, waiting for transfers between devices, shards(): lax.all_gather(wdown, 'cell', axis=0, tiled=True)  139 us
    all_gather x1, waiting for transfers between devices, shards(): lax.all_gather(wup, 'cell', axis=1, tiled=True)  106 us
    unnamed x13, waiting for transfers between devices  86.5 us
    all_to_all x2, waiting for transfers between devices, sent_and_summed(): lax.all_to_all(parts, axis, split_axis=0, concat_axis=0, tiled=True)  75 us
    all_gather x1, waiting for transfers between devices, shards(): lax.all_gather(wqkv, 'seq', axis=0, tiled=True)  55.4 us
    psum x1, waiting for transfers between devices, shards(): lax.psum(cell_up.astype(jnp.bfloat16), 'seq').astype(jnp.float32)  54.1 us
  transfers between devices with their start and end apart: 18, of which 14 were waited for; matrix products, arithmetic and copies ran while one was open for 17% of the time, Pallas kernels for 0%

profile of v1, /device:TPU:0, one launch (start us, length us, event | category | flops | bytes accessed | tf_op | source)
XLA Modules:
  0.0 1489.7 jit_solution(8222291721497306275)
XLA Ops:
  11.5 55.4 %all-gather.5.cloned.1.call-done = bf16[1120,3360]{1,0:T(8,128)(2,1)} async-done(((bf16[280,3360]{1,0:T(8,128)(2,1)}), bf16[1120,3360]{1,0:T(8,128)(2,1)}) %all-gather.5.cloned.1.call-update) | async-done | bytes 7526416 | tf_op jit(solution)/shard_map/all_gather | solution.py:202
  67.0 7.2 fusion.6
  81.6 29.2 %all-to-all-done = bf16[256,3,4,280]{0,3,1,2:T(8,128)(2,1)S(1)} async-done(((bf16[256,3,4,280]{0,3,1,2:T(8,128)(2,1)}), bf16[256,3,4,280]{0,3,1,2:T(8,128)(2,1)S(1)}, u32[]{:S(2)}, u32[]{:S(2)}) %all-to-all-start) | async-done | bytes 1720352 | tf_op jit(solution)/shard_map/all_to_all | solution.py:207
  131.0 9.3 all-to-all-done.1
  148.6 105.9 %all-gather.9.cloned.1.call-done = bf16[1120,4480]{0,1:T(8,128)(2,1)} async-done(((bf16[1120,560]{0,1:T(8,128)(2,1)}), bf16[1120,4480]{0,1:T(8,128)(2,1)}) %all-gather.9.cloned.1.call-update) | async-done | bytes 10035216 | tf_op jit(solution)/shard_map/all_gather | solution.py:228
  254.4 9.8 convolution_add_fusion
  264.2 138.9 %all-gather.11.cloned.1.call-done = bf16[4480,1120]{1,0:T(8,128)(2,1)} async-done(((bf16[560,1120]{1,0:T(8,128)(2,1)}), bf16[4480,1120]{1,0:T(8,128)(2,1)}) %all-gather.11.cloned.1.call-update) | async-done | bytes 10035216 | tf_op jit(solution)/shard_map/all_gather | solution.py:229
  403.2 12.5 fusion.105
  415.7 10.1 multiply_reduce_fusion.2
  435.3 6.7 all-to-all-done.2
  473.3 5.8 fusion.33
  481.9 10.3 collective-permute-done.2
  492.2 8.8 collective-permute-done.1
  509.0 14.6 fusion.96
  524.7 13.4 fusion.73
  541.6 6.2 reduce.20
  555.1 20.4 %reduce-scatter.14.cloned.1.call-done = bf16[280,3360]{1,0:T(8,128)(2,1)} async-done(((bf16[1120,3360]{1,0:T(8,128)(2,1)}), bf16[280,3360]{1,0:T(8,128)(2,1)}) %reduce-scatter.14.cloned.1.call-update) | async-done | bytes 1881616
  581.0 5.6 convert_element_type.245
  586.6 42.0 %reduce.19 = bf16[8,117600]{1,0:T(8,128)(2,1)} reduce(bf16[8,1,117600]{2,1,0:T(2,128)(2,1)} %convert_element_type.245, bf16[]{:T(256)} %broadcast.377), dimensions={1}, to_apply=%convert_element_type.245.reduce_sub_computation | reduce | bytes 3763202 | tf_op jit(solution)/shard_map/convert_element_type | solution.py:325
  633.2 5.5 all-to-all-start.3
  653.0 75.0 %all-to-all-done.3 = bf16[8,2,58800]{2,1,0:T(2,128)(2,1)} async-done(((bf16[8,2,58800]{2,1,0:T(2,128)(2,1)}), bf16[8,2,58800]{2,1,0:T(2,128)(2,1)}, u32[]{:S(2)}, u32[]{:S(2)}) %all-to-all-start.3) | async-done | bytes 1881632 | tf_op jit(solution)/shard_map/all_to_all | solution.py:48
  728.0 7.9 reshape.537
  735.9 5.8 reduce_sum.244
  748.0 11.3 fusion.23
  761.4 5.9 fusion.62
  768.7 189.3 %reduce-scatter.10.cloned.1.call-done = f32[1120,560]{0,1:T(8,128)} async-done(((f32[1120,4480]{0,1:T(8,128)}), f32[1120,560]{0,1:T(8,128)}) %reduce-scatter.10.cloned.1.call-update) | async-done | bytes 2508816 | tf_op jit(solution)/shard_map/reduce_scatter | solution.py:341
  960.9 337.0 %reduce-scatter.12.cloned.1.call-done = f32[560,1120]{1,0:T(8,128)} async-done(((f32[4480,1120]{1,0:T(8,128)}), f32[560,1120]{1,0:T(8,128)}) %reduce-scatter.12.cloned.1.call-update) | async-done | bytes 2508816 | tf_op jit(solution)/shard_map/reduce_scatter | solution.py:342
  1301.6 12.6 all-reduce.18
  1315.0 38.1 %all-reduce.16 = (f32[16,280]{1,0:T(8,128)}, f32[280]{0:T(512)}, f32[280]{0:T(512)}, f32[280]{0:T(512)}, f32[280]{0:T(512)}, /*index=5*/f32[280]{0:T(512)}, f32[...) all-reduce(f32[16,280]{1,0:T(8,128)S(1)} %dynamic-slice_convert_fus, ...), channel_id=1, replica_groups=mesh['cell'=8,'seq'=4] {'cell'}, use_global_device_ids=true, to_apply=%region_16.17 | all-reduce | flops 7840 | bytes 62720 | tf_op jit(solution)/shard_map/psum | solution.py:338
  1353.1 63.4 %all-reduce.23.cloned.1.call-done = (bf16[940800]{0:T(1024)(128)(2,1)}, bf16[313600]{0:T(1024)(128)(2,1)}) async-done(((bf16[940800]{0:T(1024)(128)(2,1)}, bf16[313600]{0:T(1024)(128)(2,1)}), (bf16[940800]{0:T(1024)(128)(2,1)}, bf16[313600]{0:T(1024)(128)(2,1)})) %all-reduce.23.cloned.1.call-update) | async-done | bytes 2508816
  1416.5 5.5 reshape.492
  1423.8 54.1 %all-reduce.25.cloned.1.call-done = (bf16[1120,560]{0,1:T(8,128)(2,1)}, bf16[560,1120]{1,0:T(8,128)(2,1)}) async-done(((bf16[1120,560]{0,1:T(8,128)(2,1)}, bf16[560,1120]{1,0:T(8,128)(2,1)}), (bf16[1120,560]{0,1:T(8,128)(2,1)}, bf16[560,1120]{1,0:T(8,128)(2,1)})) %all-reduce.25.cloned.1.call-update) | async-done | bytes 2508816 | tf_op jit(solution)/shard_map/psum | solution.py:345
  (254 shorter events, 146.9 us)
Async XLA Ops:
  7.2 59.7 %all-gather.5.cloned.1.call-start = ((), (), s32[]{:S(2)}) async-start(), calls=%async_computation.9 | async-start | bytes 9676800 | tf_op jit(solution)/shard_map/all_gather | solution.py:202
  8.0 59.0 %copy-start.38 = (f32[1120]{0:T(1024)S(1)}, f32[1120]{0:T(1024)}, u32[]{:S(2)}) copy-start(f32[1120]{0:T(1024)} %param.39) | copy-start | bytes 13444
  8.0 59.0 %copy-start.39 = (f32[1120]{0:T(1024)S(1)}, f32[1120]{0:T(1024)}, u32[]{:S(2)}) copy-start(f32[1120]{0:T(1024)} %param.40) | copy-start | bytes 13444
  8.0 137.0 %all-gather.7.cloned.1.call-start = ((), (), s32[]{:S(2)}) async-start(), calls=%async_computation.10 | async-start | bytes 3225600 | tf_op jit(solution)/shard_map/all_gather | solution.py:203
  8.7 245.7 %all-gather.9.cloned.1.call-start = ((), (), s32[]{:S(2)}) async-start(), calls=%async_computation.11 | async-start | bytes 11612160 | tf_op jit(solution)/shard_map/all_gather | solution.py:228
  9.5 393.7 %all-gather.11.cloned.1.call-start = ((), (), s32[]{:S(2)}) async-start(), calls=%async_computation.12 | async-start | bytes 11612160 | tf_op jit(solution)/shard_map/all_gather | solution.py:229
  11.5 62.7 %copy-start.42 = (f32[256]{0:T(256)}, f32[256]{0:T(256)S(1)}, u32[]{:S(2)}) copy-start(f32[256]{0:T(256)S(1)} %add_rsqrt_fusion.1) | copy-start | bytes 3076
  75.5 35.3 %all-to-all-start = ((bf16[256,3,4,280]{0,3,1,2:T(8,128)(2,1)}), bf16[256,3,4,280]{0,3,1,2:T(8,128)(2,1)S(1)}, u32[]{:S(2)}, u32[]{:S(2)}) async-start(bf16[256,3,4,280]{0,3,1,2:T(8,128)(2,1)} %copy.90), calls=%async_computation | async-start | bytes 3440640 | tf_op jit(solution)/shard_map/all_to_all | solution.py:207
  127.3 12.9 all-to-all-start.1
  145.0 109.5 %copy-start.36 = (f32[1120]{0:T(1024)S(1)}, f32[1120]{0:T(1024)}, u32[]{:S(2)}) copy-start(f32[1120]{0:T(1024)} %param.41) | copy-start | bytes 13444
  145.0 109.4 %copy-start.37 = (f32[1120]{0:T(1024)S(1)}, f32[1120]{0:T(1024)}, u32[]{:S(2)}) copy-start(f32[1120]{0:T(1024)} %param.42) | copy-start | bytes 13444
  145.0 109.4 %copy-start.51 = (f32[4480]{0:T(1024)S(1)}, f32[4480]{0:T(1024)}, u32[]{:S(2)}) copy-start(f32[4480]{0:T(1024)} %param.44) | copy-start | bytes 53764
  148.3 277.5 %copy-start.8 = (f32[256,1120]{0,1:T(8,128)}, f32[256,1120]{0,1:T(8,128)S(1)}, u32[]{:S(2)}) copy-start(f32[256,1120]{0,1:T(8,128)S(1)} %get-tuple-element.135) | copy-start | bytes 3440644
  148.5 277.3 %copy-start.40 = (f32[256]{0:T(256)}, f32[256]{0:T(256)S(1)}, u32[]{:S(2)}) copy-start(f32[256]{0:T(256)S(1)} %add_rsqrt_fusion) | copy-start | bytes 3076
  148.5 254.6 %copy-start.13 = (bf16[1,256,1120]{1,2,0:T(8,128)(2,1)S(1)}, bf16[1,256,1120]{1,2,0:T(8,128)(2,1)}, u32[]{:S(2)}) copy-start(bf16[1,256,1120]{1,2,0:T(8,128)(2,1)} %param.47) | copy-start | bytes 1720324
  415.7 10.1 copy-start.25
  429.3 12.8 all-to-all-start.2
  432.7 105.4 %reduce-scatter.16.cloned.1.call-start = ((), (), s32[]{:S(2)}) async-start(), calls=%async_computation.16 | async-start | bytes 3225600
  435.3 8.3 copy-start.33
  435.3 140.3 %reduce-scatter.14.cloned.1.call-start = ((), (), s32[]{:S(2)}) async-start(), calls=%async_computation.15 | async-start | bytes 9676800
  443.7 8.9 slice-start
  443.7 8.9 slice-start.1
  479.9 12.3 collective-permute-start.2
  480.2 20.8 %collective-permute-start.1 = (bf16[256,3,1,280]{0,3,2,1:T(8,128)(2,1)S(1)}, bf16[256,3,1,280]{0,3,2,1:T(8,128)(2,1)S(1)}, u32[]{:S(2)}, u32[]{:S(2)}) collective-permute-start(bf16[256,3,1,280]{0,3,2,1:T(8,128)(2,1)S(1)} %get-tuple-element.120), channel_id=1, source_target_pairs={{0,2},{1,3},{2,0},{3,1},{4,6},{5,7},{6,4},{7,5},{8,10},{9,11},{10,... | collective-permute-start | bytes 1290248 | tf_op jit(solution)/shard_map/ppermute | solution.py:31
  481.3 19.8 %collective-permute-start = (bf16[256,3,1,280]{0,3,2,1:T(8,128)(2,1)S(1)}, bf16[256,3,1,280]{0,3,2,1:T(8,128)(2,1)S(1)}, u32[]{:S(2)}, u32[]{:S(2)}) collective-permute-start(bf16[256,3,1,280]{0,3,2,1:T(8,128)(2,1)S(1)} %get-tuple-element.121), channel_id=1, source_target_pairs={{0,1},{1,0},{2,3},{3,2},{4,5},{5,4},{6,7},{7,6},{8,9},{9,8},{10,11... | collective-permute-start | bytes 1290248 | tf_op jit(solution)/shard_map/ppermute | solution.py:31
  507.8 450.2 %reduce-scatter.10.cloned.1.call-start = ((), (), s32[]{:S(2)}) async-start(), calls=%async_computation.13 | async-start | bytes 23224320 | tf_op jit(solution)/shard_map/reduce_scatter | solution.py:341
  523.6 774.3 %reduce-scatter.12.cloned.1.call-start = ((), (), s32[]{:S(2)}) async-start(), calls=%async_computation.14 | async-start | bytes 23224320 | tf_op jit(solution)/shard_map/reduce_scatter | solution.py:342
  550.3 82.9 %all-to-all-start.4 = ((bf16[8,2,19600]{2,1,0:T(2,128)(2,1)}), bf16[8,2,19600]{2,1,0:T(2,128)(2,1)}, u32[]{:S(2)}, u32[]{:S(2)}) async-start(bf16[8,2,19600]{2,1,0:T(2,128)(2,1)} %reshape.538), calls=%async_computation.4 | async-start | bytes 1261568 | tf_op jit(solution)/shard_map/all_to_all | solution.py:48
  633.2 94.8 %all-to-all-start.3 = ((bf16[8,2,58800]{2,1,0:T(2,128)(2,1)}), bf16[8,2,58800]{2,1,0:T(2,128)(2,1)}, u32[]{:S(2)}, u32[]{:S(2)}) async-start(bf16[8,2,58800]{2,1,0:T(2,128)(2,1)} %reshape.536), calls=%async_computation.3 | async-start | bytes 3768320 | tf_op jit(solution)/shard_map/all_to_all | solution.py:48
  638.7 777.8 %all-reduce.23.cloned.1.call-start = ((), (), s32[]{:S(2)}) async-start(), calls=%async_computation.17 | async-start | bytes 5021696
  747.8 730.1 %all-reduce.25.cloned.1.call-start = ((), (), s32[]{:S(2)}) async-start(), calls=%async_computation.18 | async-start | bytes 5160960 | tf_op jit(solution)/shard_map/psum | solution.py:345
  960.9 340.0 %copy-start.12 = (f32[256,3360]{0,1:T(8,128)S(1)}, f32[256,3360]{0,1:T(8,128)}, u32[]{:S(2)}) copy-start(f32[256,3360]{0,1:T(8,128)} %convert_element_type.222) | copy-start | bytes 10321924
  (45 other events, 154.3 us)
Sparse Core Ops, SparseCore 0:
  9.6 57.3 all-gather.4
  68.5 34.8 all-gather.6
  105.6 148.7 all-gather.8
  256.4 146.6 all-gather.10
  436.4 33.1 reduce-scatter.15
  507.9 67.5 reduce-scatter.13
  579.4 378.5 reduce-scatter.9
  961.9 335.9 reduce-scatter.11
  1302.8 113.6 all-reduce.22
  1419.5 58.4 all-reduce.24
